TPU v7x, 32 devices: a whole 2x2x4 slice. The times are simulated.
32 devices in a mesh: row: 8 (over z, x), col: 4 (over y, core).
Axes of the slice: x: 2, y: 2, z: 4, core: 2. Of those that a mesh axis runs over, the one named last changes fastest.
Arguments:
- eigvecs: float32 [16384, 4096], P('row', 'col'), may hold values from -6 to 6
- reflectors: float32 [2, 16384, 256], P(None, ('row', 'col')), may hold values from -0.13258252 to 0.13258252
- tfactors: float32 [2, 256, 256], replicated, may hold values from -1 to 2, as said below
Outputs:
- back: float32 [16384, 4096], P('row', 'col')
Inputs may be any that keep to these rules, and one draw needn't show every extreme that they name: Each tfactors[p] is upper triangular; its diagonal lies between 0.3 and 1.9.
All inputs are finite; a program needn't handle non-finite values.
Results may differ from a plain program's by a relative error of at most 0.00014.
Values sent between devices are 32-bit elements; how exact they have to be, the bound alone decides.
A program may use at most 128 MiB of HBM per device.

v0:
```python
import jax
import jax.numpy as jnp
from jax import lax
from jax.sharding import PartitionSpec as P

exact_mode = lax.Precision.HIGHEST


def product(left, right):
    return jnp.dot(left, right, precision=exact_mode, preferred_element_type=jnp.float32)


def left_contract(block, current):
    return lax.dot_general(
        block,
        current,
        (((0,), (0,)), ((), ())),
        precision=exact_mode,
        preferred_element_type=jnp.float32,
    )


def local(eigvecs, reflectors, tfactors):
    gathered = lax.all_gather(reflectors, "col", axis=1, tiled=True)
    lower_refl = gathered[0]
    upper_refl = gathered[1]
    joint_part = jnp.einsum(
        "prn,rk->pnk", gathered, eigvecs, precision=exact_mode, preferred_element_type=jnp.float32
    )
    gram_part = left_contract(lower_refl, upper_refl)
    inner_prod, gram_sum = lax.psum((joint_part, gram_part), "row")
    coeff_high = product(tfactors[1], inner_prod[1])
    coeff_low = product(tfactors[0], inner_prod[0] - product(gram_sum, coeff_high))
    stacked = jnp.stack([coeff_low, coeff_high])
    update = jnp.einsum(
        "prn,pnk->rk", gathered, stacked, precision=exact_mode, preferred_element_type=jnp.float32
    )
    return eigvecs - update


def solution(mesh):
    return jax.shard_map(
        local,
        mesh=mesh,
        in_specs=(P("row", "col"), P(None, ("row", "col"), None), P()),
        out_specs=P("row", "col"),
        check_vma=False,
    )
```

profile of v0, /device:TPU:0, one launch (start us, length us, event | category | flops | bytes accessed | tf_op | source)
XLA Modules:
  0.0 218.5 jit_solution(17570545092156415697)
XLA Ops:
  6.5 0.0 all-gather.2.cloned.1.call-start
  6.5 2.5 %copy.4 = f32[2,512,256]{1,2,0:T(8,128)} copy(f32[2,512,256]{2,1,0:T(8,128)} %param.4) | data formatting | bytes 2097152 | tf_op args[1]
  9.1 0.0 all-gather.2.cloned.1.call-update
  9.1 0.0 all-reduce.3.cloned.1.call-start
  9.1 37.3 %all-gather.2.cloned.1.call-done = f32[2,2048,256]{1,2,0:T(8,128)} async-done(((f32[2,512,256]{1,2,0:T(8,128)}), f32[2,2048,256]{1,2,0:T(8,128)}) %all-gather.2.cloned.1.call-update) | async-done | bytes 4194320 | tf_op jit(solution)/shard_map/all_gather | solution.py:24
  46.4 0.0 copy-start
  46.4 4.9 %fusion.2 = f32[256,256]{1,0:T(8,128)} fusion(f32[2,2048,256]{1,2,0:T(8,128)} %all-gather.2.cloned.1.call-done), kind=kOutput, calls=%fused_computation.4 | convolution fusion | flops 1610612736 | bytes 4456448 | tf_op jit(solution)/shard_map/dot_general | solution.py:14
  51.4 0.0 copy-done
  51.4 16.9 %fusion = f32[2,256,1024]{2,1,0:T(8,128)} fusion(f32[2,2048,256]{1,2,0:T(8,128)S(1)} %copy-done, f32[2048,1024]{1,0:T(8,128)} %param.3), kind=kOutput, calls=%fused_computation.1 | convolution fusion | flops 12884901888 | bytes 14680064 | tf_op jit(solution)/shard_map/prn,rk->pnk/dot_general | solution.py:27
  68.3 0.0 all-reduce.3.cloned.1.call-update
  68.4 0.0 copy-start.2
  68.4 9.2 %copy.6 = f32[2048,1024]{0,1:T(8,128)} copy(f32[2048,1024]{1,0:T(8,128)} %param.3) | data formatting | bytes 16777216 | tf_op args[0]
  77.6 99.5 %all-reduce.3.cloned.1.call-done = (f32[2,256,1024]{2,1,0:T(8,128)}, f32[256,256]{1,0:T(8,128)}) async-done(((f32[2,256,1024]{2,1,0:T(8,128)}, f32[256,256]{1,0:T(8,128)}), (f32[2,256,1024]{2,1,0:T(8,128)}, f32[256,256]{1,0:T(8,128)})) %all-reduce.3.cloned.1.call-update) | async-done | bytes 2359312 | tf_op jit(solution)/shard_map/psum | solution.py:31
  177.1 0.0 copy-start.1
  177.1 0.0 copy-done.2
  177.1 3.2 %fusion.6 = f32[1024,256]{1,0:T(8,128)S(1)} fusion(f32[2,256,1024]{2,1,0:T(8,128)} %get-tuple-element.5, f32[2,256,256]{2,1,0:T(8,128)S(1)} %copy-done.2), kind=kOutput, calls=%fused_computation.12 | convolution fusion | flops 805306368 | bytes 2359296 | tf_op jit(solution)/shard_map/dot_general | solution.py:10
  180.3 2.4 %convolution_subtract_fusion = f32[256,1024]{1,0:T(8,128)S(1)} fusion(f32[256,256]{1,0:T(8,128)} %get-tuple-element.6, f32[1024,256]{1,0:T(8,128)S(1)} %fusion.6, f32[2,256,1024]{2,1,0:T(8,128)} %get-tuple-element.5), kind=kOutput, calls=%fused_computation.10 | convolution fusion | flops 805568512 | bytes 3407872 | tf_op jit(solution)/shard_map/dot_general | solution.py:10
  182.7 1.8 convolution_bitcast_fusion
  184.5 0.0 copy-done.1
  184.5 17.9 %bitcast_subtract_fusion = f32[2048,1024]{0,1:T(8,128)} fusion(f32[2048,1024]{0,1:T(8,128)} %copy.6, f32[2,2048,256]{1,2,0:T(8,128)S(1)} %copy-done.1, f32[1,256,1024]{1,2,0:T(8,128)S(1)} %bitcast.38, f32[1,256,1024]{1,2,0:T(8,128)S(1)} %convolution_bitcast_fusion), kind=kOutput, calls=%fused_computation | convolution fusion | flops 12887523328 | bytes 23068672 | tf_op jit(solution)/shard_map/prn,pnk->rk/dot_general | solution.py:35
  202.4 9.2 %copy.7 = f32[2048,1024]{1,0:T(8,128)} copy(f32[2048,1024]{0,1:T(8,128)} %bitcast_subtract_fusion) | data formatting | bytes 16777216 | tf_op jit(solution)/shard_map/sub | solution.py:38
Async XLA Ops:
  6.5 39.9 %all-gather.2.cloned.1.call-start = ((), (), s32[]{:S(2)}) async-start(), calls=%async_computation | async-start | bytes 5242880 | tf_op jit(solution)/shard_map/all_gather | solution.py:24
  9.1 168.0 %all-reduce.3.cloned.1.call-start = ((), (), s32[]{:S(2)}) async-start(), calls=%async_computation.1 | async-start | bytes 4718592 | tf_op jit(solution)/shard_map/psum | solution.py:31
  46.4 5.0 %copy-start = (f32[2,2048,256]{1,2,0:T(8,128)S(1)}, f32[2,2048,256]{1,2,0:T(8,128)}, u32[]{:S(2)}) copy-start(f32[2,2048,256]{1,2,0:T(8,128)} %all-gather.2.cloned.1.call-done) | copy-start | bytes 12582916
  68.4 108.8 %copy-start.2 = (f32[2,256,256]{2,1,0:T(8,128)S(1)}, f32[2,256,256]{2,1,0:T(8,128)}, u32[]{:S(2)}) copy-start(f32[2,256,256]{2,1,0:T(8,128)} %param.5) | copy-start | bytes 1572868
  177.1 7.4 %copy-start.1 = (f32[2,2048,256]{1,2,0:T(8,128)S(1)}, f32[2,2048,256]{1,2,0:T(8,128)}, u32[]{:S(2)}) copy-start(f32[2,2048,256]{1,2,0:T(8,128)} %all-gather.2.cloned.1.call-done) | copy-start | bytes 12582916
Sparse Core Ops, SparseCore 0:
  9.2 37.1 all-gather.1
  68.5 108.6 all-reduce.2
where the time goes:
time: 219 us
  waiting for transfers between devices  137 us (63%)
  matrix products  47.2 us (22%)
  local copies, waits for them, and re-layouts  21 us (10%)
  between operations  13.4 us (6%)
    psum x1, waiting for transfers between devices, local(): inner_prod, gram_sum = lax.psum((joint_part, gram_part), 'row')  99.5 us
    all_gather x1, waiting for transfers between devices, local(): gathered = lax.all_gather(reflectors, 'col', axis=1, tiled=True)  37.3 us
    dot_general x1, matrix products, local(): jnp.einsum('prn,pnk->rk', gathered, stacked, precision=exact_mode, prefer...  17.9 us
    dot_general x1, matrix products, local(): jnp.einsum('prn,rk->pnk', gathered, eigvecs, precision=exact_mode, prefer...  16.9 us
    unnamed x8, local copies, waits for them, and re-layouts  11.8 us
    sub x1, local copies, waits for them, and re-layouts, local(): return eigvecs - update  9.24 us
    dot_general x3, matrix products, product(): jnp.dot(left, right, precision=exact_mode, preferred_element_type=jnp.flo...  7.36 us
    dot_general x1, matrix products, left_contract(): lax.dot_general(block, current, (((0,), (0,)), ((), ())), precision=exact...  4.95 us
  transfers between devices with their start and end apart: 2, of which 2 were waited for; matrix products, arithmetic and copies ran while one was open for 4% of the time, Pallas kernels for 0%

commit v1 on v0

v1 whole, which is shorter than its diff:
```python
import functools

import jax
import jax.numpy as jnp
from jax import lax
from jax.experimental import pallas as pl
from jax.experimental.pallas import tpu as pltpu
from jax.sharding import PartitionSpec as P

F32 = jnp.float32
BF16 = jnp.bfloat16
MESH = pl.DeviceIdType.MESH
TILE = 256


def halves(value):
    high = value.astype(BF16)
    return high, (value - high.astype(F32)).astype(BF16)


def dot3(left, right, contract=((1,), (0,))):
    def one(a, b):
        return lax.dot_general(a, b, (contract, ((), ())), preferred_element_type=F32)

    return one(left[0], right[0]) + (one(left[0], right[1]) + one(left[1], right[0]))


def flip(index, bit):
    return index + (1 - 2 * ((index // bit) % 2)) * bit


def reduce_kernel(rows_n, cols_n, cw, eig, refl, tfac, vhi_out, vlo_out, chi, clo,
                  ebuf, ehi, elo, vbuf, vhi, vlo, g_hi, g_lo, r_hi, r_lo, a_hi, a_lo,
                  load_e, load_v, store_v, v_send, v_recv, rs_send, rs_recv, ag_send, ag_recv):
    row, col = lax.axis_index("row"), lax.axis_index("col")
    panels, part, nb = refl.shape
    block, width = eig.shape
    per = nb // cw
    chunks = panels * per
    row_bits = rows_n.bit_length() - 1
    col_bits = cols_n.bit_length() - 1
    tiles = block // TILE

    def place(k):
        return (1, k) if k < per else (0, k - per)

    def own_load(k):
        panel, part_at = place(k)
        return pltpu.make_async_copy(
            refl.at[panel, :, pl.ds(part_at * cw, cw)], vbuf.at[k, col], load_v.at[k])

    def e_load(t):
        return pltpu.make_async_copy(
            eig.at[pl.ds(t * TILE, TILE), :], ebuf.at[pl.ds(t * TILE, TILE), :], load_e.at[t])

    for k in range(chunks):
        own_load(k).start()
    for t in range(tiles):
        e_load(t).start()

    barrier = pltpu.get_barrier_semaphore()
    for b in range(row_bits):
        pl.semaphore_signal(barrier, inc=1, device_id=(flip(row, 1 << b), col), device_id_type=MESH)
    for b in range(col_bits):
        pl.semaphore_signal(barrier, inc=1, device_id=(row, flip(col, 1 << b)), device_id_type=MESH)
    pl.semaphore_wait(barrier, row_bits + col_bits)

    def rel(r):
        at = col
        for b in range(col_bits):
            if (r >> b) & 1:
                at = flip(at, 1 << b)
        return at

    def v_copy(k, r, b):
        slot = vbuf.at[k, rel(r)]
        return pltpu.make_async_remote_copy(
            src_ref=slot, dst_ref=slot, send_sem=v_send.at[k, r + (1 << b)],
            recv_sem=v_recv.at[k, r + (1 << b)],
            device_id=(row, flip(col, 1 << b)), device_id_type=MESH)

    def v_arrived(k, r):
        low = (r & -r).bit_length() - 1
        slot = vbuf.at[k, rel(r)]
        pltpu.make_async_remote_copy(
            src_ref=slot, dst_ref=slot, send_sem=v_send.at[k, r], recv_sem=v_recv.at[k, r],
            device_id=(row, flip(col, 1 << low)), device_id_type=MESH).wait_recv()

    for k in range(chunks):
        own_load(k).wait()
        for b in reversed(range(col_bits)):
            v_copy(k, 0, b).start()

    for t in range(tiles):
        e_load(t).wait()

    @pl.loop(0, tiles)
    def _(t):
        at = pl.ds(pl.multiple_of(t * TILE, TILE), TILE)
        high, low = halves(ebuf[at, :])
        ehi[at, :] = high
        elo[at, :] = low

    order = sorted(range(1, cols_n), key=lambda r: (-(r & -r), r))

    def buffers(k):
        panel, part_at = place(k)
        g, r, a = (g_hi, r_hi, a_hi) if panel == 1 else (g_lo, r_lo, a_lo)
        return g, r, a, part_at * cw

    def contract(k):
        panel, part_at = place(k)
        for r in order:
            v_arrived(k, r)
            for b in reversed(range((r & -r).bit_length() - 1)):
                v_copy(k, r, b).start()
        lane = panel * nb + part_at * cw
        here = slice(lane, lane + cw)

        for c in range(cols_n):
            high, low = halves(vbuf[k, c])
            vhi[c * part:(c + 1) * part, here] = high
            vlo[c * part:(c + 1) * part, here] = low
        g, _, _, base = buffers(k)
        left = vhi[:, here], vlo[:, here]

        @pl.loop(0, width // TILE)
        def _(n):
            at = pl.ds(pl.multiple_of(n * TILE, TILE), TILE)
            g[base:base + cw, at] = dot3(left, (ehi[:, at], elo[:, at]), ((0,), (0,)))

        if panel == 0:
            upper = slice(nb, 2 * nb)
            g[base:base + cw, width:width + nb] = dot3(left, (vhi[:, upper], vlo[:, upper]), ((0,), (0,)))

    def start_of(level):
        at = 0
        for b in range(level):
            at = at + ((row // (1 << b)) % 2) * (cw >> (b + 1))
        return at

    def rs_copy(k, level):
        g, r, _, base = buffers(k)
        half = cw >> (level + 1)
        bit = (row // (1 << level)) % 2
        src = pl.multiple_of(base + start_of(level) + (1 - bit) * half, 8)
        dst = base + cw - 2 * half
        return pltpu.make_async_remote_copy(
            src_ref=g.at[pl.ds(src, half), :], dst_ref=r.at[pl.ds(dst, half), :],
            send_sem=rs_send.at[k, level], recv_sem=rs_recv.at[k, level],
            device_id=(flip(row, 1 << level), col), device_id_type=MESH)

    def rs_take(k, level):
        g, r, a, base = buffers(k)
        rs_copy(k, level).wait_recv()
        half = cw >> (level + 1)
        keep = pl.ds(pl.multiple_of(base + start_of(level + 1), 8), half)
        came = base + cw - 2 * half
        total = g[keep, :] + r[came:came + half, :]
        if level == row_bits - 1:
            a[keep, :] = total
        else:
            g[keep, :] = total

    def ag_copy(k, level):
        _, _, a, base = buffers(k)
        size = cw >> (level + 1)
        rows = pl.ds(pl.multiple_of(base + start_of(level + 1), 8), size)
        return pltpu.make_async_remote_copy(
            src_ref=a.at[rows, :], dst_ref=a.at[rows, :],
            send_sem=ag_send.at[k, level], recv_sem=ag_recv.at[k, level],
            device_id=(flip(row, 1 << level), col), device_id_type=MESH)

    def ag_take(k, level):
        _, _, a, base = buffers(k)
        size = cw >> (level + 1)
        bit = (row // (1 << level)) % 2
        rows = pl.ds(pl.multiple_of(base + start_of(level) + (1 - bit) * size, 8), size)
        pltpu.make_async_remote_copy(
            src_ref=a.at[rows, :], dst_ref=a.at[rows, :],
            send_sem=ag_send.at[k, level], recv_sem=ag_recv.at[k, level],
            device_id=(flip(row, 1 << level), col), device_id_type=MESH).wait_recv()

    def stage(k, s):
        if s == 0:
            contract(k)
            rs_copy(k, 0).start()
        elif s < row_bits:
            rs_take(k, s - 1)
            rs_copy(k, s).start()
        elif s == row_bits:
            rs_take(k, s - 1)
            ag_copy(k, row_bits - 1).start()
        else:
            level = 2 * row_bits - s
            ag_take(k, level)
            if level:
                ag_copy(k, level - 1).start()

    stages = 2 * row_bits + 1
    for slot in range(chunks + stages - 1):
        for k in range(chunks):
            if 0 <= slot - k < stages:
                stage(k, slot - k)
        if slot == chunks - 1:
            keep_hi = pltpu.make_async_copy(vhi, vhi_out, store_v.at[0])
            keep_lo = pltpu.make_async_copy(vlo, vlo_out, store_v.at[1])
            keep_hi.start()
            keep_lo.start()

    upper_t, lower_t = halves(tfac[1]), halves(tfac[0])
    gram = halves(a_lo[:, width:width + nb])

    @pl.loop(0, width // TILE)
    def _(n):
        at = pl.ds(pl.multiple_of(n * TILE, TILE), TILE)
        high = halves(dot3(upper_t, halves(a_hi[:, at])))
        low = halves(dot3(lower_t, halves(a_lo[:, at] - dot3(gram, high))))
        chi[0:nb, at] = low[0]
        clo[0:nb, at] = low[1]
        chi[nb:2 * nb, at] = high[0]
        clo[nb:2 * nb, at] = high[1]

    for k in range(chunks):
        for r in range(cols_n):
            low = (r & -r).bit_length() - 1 if r else col_bits
            for b in range(low):
                v_copy(k, r, b).wait_send()
        for level in range(row_bits):
            rs_copy(k, level).wait_send()
            ag_copy(k, level).wait_send()
    keep_hi.wait()
    keep_lo.wait()


def update_kernel(eig, vhi, vlo, chi, clo, out):
    out[...] = eig[...] - dot3((vhi[...], vlo[...]), (chi[...], clo[...]))


def local(rows_n, cols_n, eigvecs, reflectors, tfactors):
    panels, part, nb = reflectors.shape
    block, width = eigvecs.shape
    cw = max(128, 8 * rows_n)
    chunks = panels * nb // cw
    row_bits = rows_n.bit_length() - 1
    total = panels * nb
    anywhere = pl.BlockSpec(memory_space=pl.ANY)
    vmem = pl.BlockSpec(memory_space=pltpu.VMEM)
    dma = pltpu.SemaphoreType.DMA
    pair = lambda: [pltpu.VMEM((nb, width), F32), pltpu.VMEM((nb, width + nb), F32)]
    vhi, vlo, chi, clo = pl.pallas_call(
        functools.partial(reduce_kernel, rows_n, cols_n, cw),
        out_shape=[jax.ShapeDtypeStruct((block, total), BF16)] * 2
        + [jax.ShapeDtypeStruct((total, width), BF16)] * 2,
        in_specs=[anywhere, anywhere, vmem],
        out_specs=[anywhere, anywhere, vmem, vmem],
        scratch_shapes=[
            pltpu.VMEM((block, width), F32),
            pltpu.VMEM((block, width), BF16),
            pltpu.VMEM((block, width), BF16),
            pltpu.VMEM((chunks, cols_n, part, cw), F32),
            pltpu.VMEM((block, total), BF16),
            pltpu.VMEM((block, total), BF16),
            *pair(), *pair(), *pair(),
            dma((block // TILE,)), dma((chunks,)), dma((2,)),
            dma((chunks, cols_n)), dma((chunks, cols_n)),
            dma((chunks, row_bits)), dma((chunks, row_bits)),
            dma((chunks, row_bits)), dma((chunks, row_bits)),
        ],
        compiler_params=pltpu.CompilerParams(
            collective_id=0, has_side_effects=True, vmem_limit_bytes=60 * 1024 * 1024),
    )(eigvecs, reflectors, tfactors)
    rows = 256
    return pl.pallas_call(
        update_kernel,
        grid=(block // rows,),
        out_shape=jax.ShapeDtypeStruct((block, width), F32),
        in_specs=[
            pl.BlockSpec((rows, width), lambda i: (i, 0)),
            pl.BlockSpec((rows, total), lambda i: (i, 0)),
            pl.BlockSpec((rows, total), lambda i: (i, 0)),
            pl.BlockSpec((total, width), lambda i: (0, 0)),
            pl.BlockSpec((total, width), lambda i: (0, 0)),
        ],
        out_specs=pl.BlockSpec((rows, width), lambda i: (i, 0)),
    )(eigvecs, vhi, vlo, chi, clo)


def solution(mesh):
    return jax.shard_map(
        functools.partial(local, mesh.shape["row"], mesh.shape["col"]),
        mesh=mesh,
        in_specs=(P("row", "col"), P(None, ("row", "col"), None), P()),
        out_specs=P("row", "col"),
        check_vma=False,
    )
```

time: 219 us -> 115 us (0.53)
  waiting for transfers between devices: 137 us -> 0 us
  Pallas kernels: 0 us -> 114 us
  matrix products: 47.2 us -> 0 us
  local copies, waits for them, and re-layouts: 21 us -> 0 us
  between operations: 13.4 us -> 0.01 us
    pallas_call x0 -> x2, Pallas kernels: none -> 114 us  [the longest x1 101 us: local(): pl.pallas_call(functools.partial(reduce_kernel, rows_n, cols_n, cw), out_...]
    psum x1 -> x0, waiting for transfers between devices: 99.5 us -> none  [local(): inner_prod, gram_sum = lax.psum((joint_part, gram_part), 'row')]
    dot_general x6 -> x0, matrix products: 47.2 us -> none  [the longest x1 17.9 us: local(): jnp.einsum('prn,pnk->rk', gathered, stacked, precision=exact_mode, prefer...]
    all_gather x1 -> x0, waiting for transfers between devices: 37.3 us -> none  [local(): gathered = lax.all_gather(reflectors, 'col', axis=1, tiled=True)]
    unnamed x8 -> x0, local copies, waits for them, and re-layouts: 11.8 us -> none
    sub x1 -> x0, local copies, waits for them, and re-layouts: 9.24 us -> none  [local(): return eigvecs - update]
  transfers between devices with their start and end apart: 2 -> 0, of which waited for: 2 -> 0; matrix products, arithmetic and copies ran while one was open for 4% -> 0% of each run, Pallas kernels for 0% -> 0%
where the time goes in v1:
time: 115 us; the launch traced here: 114 us
  Pallas kernels  114 us (99%)
    pallas_call x1, Pallas kernels, local(): pl.pallas_call(functools.partial(reduce_kernel, rows_n, cols_n, cw), out_...  101 us
    pallas_call x1, Pallas kernels, local(): pl.pallas_call(update_kernel, grid=(block // rows,), out_shape=jax.ShapeD...  13.6 us

profile of v1, /device:TPU:0, one launch (start us, length us, event | category | flops | bytes accessed | tf_op | source)
XLA Modules:
  0.0 114.4 jit_solution(14073176376965634275)
XLA Ops:
  0.0 100.8 %shard_map.37 = (bf16[2048,512]{1,0:T(8,128)(2,1)}, bf16[2048,512]{1,0:T(8,128)(2,1)}, bf16[512,1024]{1,0:T(8,128)(2,1)}, bf16[512,1024]{1,0:T(8,128)(2,1)}) custom-call(f32[2048,1024]{1,0:T(8,128)} %eig.3, f32[2,512,256]{2,1,0:T(8,128)} %refl.1, f32[2,256,256]{2,1,0:T(8,128)} %tfac.1), custom_call_target="tpu_custom_call" | custom-call | tf_op jit(solution)/shard_map/pallas_call | solution.py:251
  100.8 13.6 %shard_map.38 = f32[2048,1024]{1,0:T(8,128)} custom-call(f32[2048,1024]{1,0:T(8,128)} %eig.3, bf16[2048,512]{1,0:T(8,128)(2,1)} %get-tuple-element.9.vhi, bf16[2048,512]{1,0:T(8,128)(2,1)} %get-tuple-element.10.vlo, bf16[512,1024]{1,0:T(8,128)(2,1)} %get-tuple-element.11.chi, bf16[512,1024]{1,0:T(8,128)(2,1)} %get-tuple-element.12.clo), custom_call_target="tpu_custom_call" | custom-call | tf_op jit(solution)/shard_map/pallas_call | solution.py:274

commit v2 on v1

--- a/solution.py
+++ b/solution.py
@@ -108,12 +108,19 @@
         g, r, a = (g_hi, r_hi, a_hi) if panel == 1 else (g_lo, r_lo, a_lo)
         return g, r, a, part_at * cw
 
-    def contract(k):
-        panel, part_at = place(k)
-        for r in order:
+    relayed = [r for r in order if r % 2 == 0]
+    direct = [r for r in order if r % 2]
+
+    def relay(k):
+        for r in relayed:
             v_arrived(k, r)
             for b in reversed(range((r & -r).bit_length() - 1)):
                 v_copy(k, r, b).start()
+
+    def contract(k):
+        panel, part_at = place(k)
+        for r in direct:
+            v_arrived(k, r)
         lane = panel * nb + part_at * cw
         here = slice(lane, lane + cw)
 
@@ -123,85 +130,96 @@
             vlo[c * part:(c + 1) * part, here] = low
         g, _, _, base = buffers(k)
         left = vhi[:, here], vlo[:, here]
+        both = jnp.concatenate(left, axis=1)
 
         @pl.loop(0, width // TILE)
         def _(n):
             at = pl.ds(pl.multiple_of(n * TILE, TILE), TILE)
-            g[base:base + cw, at] = dot3(left, (ehi[:, at], elo[:, at]), ((0,), (0,)))
+            first = lax.dot_general(both, ehi[:, at], (((0,), (0,)), ((), ())), preferred_element_type=F32)
+            second = lax.dot_general(left[0], elo[:, at], (((0,), (0,)), ((), ())), preferred_element_type=F32)
+            g[base:base + cw, at] = first[:cw] + (first[cw:] + second)
 
         if panel == 0:
             upper = slice(nb, 2 * nb)
             g[base:base + cw, width:width + nb] = dot3(left, (vhi[:, upper], vlo[:, upper]), ((0,), (0,)))
 
-    def start_of(level):
+    upward = list(range(row_bits))
+    orders = (upward, upward[1:] + upward[:1])
+
+    def bit_of(p, level):
+        return (row // (1 << orders[p][level])) % 2
+
+    def start_of(p, level):
         at = 0
         for b in range(level):
-            at = at + ((row // (1 << b)) % 2) * (cw >> (b + 1))
+            at = at + bit_of(p, b) * (cw >> (b + 1))
         return at
 
-    def rs_copy(k, level):
+    def lanes(buffer, p):
+        middle = width // 2
+        return slice(0, middle) if p == 0 else slice(middle, buffer.shape[1])
+
+    def rs_copy(k, p, level):
         g, r, _, base = buffers(k)
         half = cw >> (level + 1)
-        bit = (row // (1 << level)) % 2
-        src = pl.multiple_of(base + start_of(level) + (1 - bit) * half, 8)
+        src = pl.multiple_of(base + start_of(p, level) + (1 - bit_of(p, level)) * half, 8)
         dst = base + cw - 2 * half
+        here = lanes(g, p)
         return pltpu.make_async_remote_copy(
-            src_ref=g.at[pl.ds(src, half), :], dst_ref=r.at[pl.ds(dst, half), :],
-            send_sem=rs_send.at[k, level], recv_sem=rs_recv.at[k, level],
-            device_id=(flip(row, 1 << level), col), device_id_type=MESH)
-
-    def rs_take(k, level):
+            src_ref=g.at[pl.ds(src, half), here], dst_ref=r.at[pl.ds(dst, half), here],
+            send_sem=rs_send.at[k, p, level], recv_sem=rs_recv.at[k, p, level],
+            device_id=(flip(row, 1 << orders[p][level]), col), device_id_type=MESH)
+
+    def rs_take(k, p, level):
         g, r, a, base = buffers(k)
-        rs_copy(k, level).wait_recv()
+        rs_copy(k, p, level).wait_recv()
         half = cw >> (level + 1)
-        keep = pl.ds(pl.multiple_of(base + start_of(level + 1), 8), half)
+        keep = pl.ds(pl.multiple_of(base + start_of(p, level + 1), 8), half)
         came = base + cw - 2 * half
-        total = g[keep, :] + r[came:came + half, :]
+        here = lanes(g, p)
+        total = g[keep, here] + r[came:came + half, here]
         if level == row_bits - 1:
-            a[keep, :] = total
+            a[keep, here] = total
         else:
-            g[keep, :] = total
-
-    def ag_copy(k, level):
+            g[keep, here] = total
+
+    def ag_at(k, p, level, mine):
         _, _, a, base = buffers(k)
         size = cw >> (level + 1)
-        rows = pl.ds(pl.multiple_of(base + start_of(level + 1), 8), size)
+        bit = bit_of(p, level) if mine else 1 - bit_of(p, level)
+        rows = pl.ds(pl.multiple_of(base + start_of(p, level) + bit * size, 8), size)
+        slot = a.at[rows, lanes(a, p)]
         return pltpu.make_async_remote_copy(
-            src_ref=a.at[rows, :], dst_ref=a.at[rows, :],
-            send_sem=ag_send.at[k, level], recv_sem=ag_recv.at[k, level],
-            device_id=(flip(row, 1 << level), col), device_id_type=MESH)
-
-    def ag_take(k, level):
-        _, _, a, base = buffers(k)
-        size = cw >> (level + 1)
-        bit = (row // (1 << level)) % 2
-        rows = pl.ds(pl.multiple_of(base + start_of(level) + (1 - bit) * size, 8), size)
-        pltpu.make_async_remote_copy(
-            src_ref=a.at[rows, :], dst_ref=a.at[rows, :],
-            send_sem=ag_send.at[k, level], recv_sem=ag_recv.at[k, level],
-            device_id=(flip(row, 1 << level), col), device_id_type=MESH).wait_recv()
+            src_ref=slot, dst_ref=slot,
+            send_sem=ag_send.at[k, p, level], recv_sem=ag_recv.at[k, p, level],
+            device_id=(flip(row, 1 << orders[p][level]), col), device_id_type=MESH)
 
     def stage(k, s):
         if s == 0:
             contract(k)
-            rs_copy(k, 0).start()
-        elif s < row_bits:
-            rs_take(k, s - 1)
-            rs_copy(k, s).start()
-        elif s == row_bits:
-            rs_take(k, s - 1)
-            ag_copy(k, row_bits - 1).start()
-        else:
-            level = 2 * row_bits - s
-            ag_take(k, level)
-            if level:
-                ag_copy(k, level - 1).start()
+        for p in range(2):
+            if s == 0:
+                rs_copy(k, p, 0).start()
+            elif s < row_bits:
+                rs_take(k, p, s - 1)
+                rs_copy(k, p, s).start()
+            elif s == row_bits:
+                rs_take(k, p, s - 1)
+                ag_at(k, p, row_bits - 1, True).start()
+            else:
+                level = 2 * row_bits - s
+                ag_at(k, p, level, False).wait_recv()
+                if level:
+                    ag_at(k, p, level - 1, True).start()
 
     stages = 2 * row_bits + 1
-    for slot in range(chunks + stages - 1):
-        for k in range(chunks):
+    relay(0)
+    for slot in range(chunks - 1 + stages):
+        for k in reversed(range(chunks)):
             if 0 <= slot - k < stages:
                 stage(k, slot - k)
+        if slot + 1 < chunks:
+            relay(slot + 1)
         if slot == chunks - 1:
             keep_hi = pltpu.make_async_copy(vhi, vhi_out, store_v.at[0])
             keep_lo = pltpu.make_async_copy(vlo, vlo_out, store_v.at[1])
@@ -226,9 +244,10 @@
             low = (r & -r).bit_length() - 1 if r else col_bits
             for b in range(low):
                 v_copy(k, r, b).wait_send()
-        for level in range(row_bits):
-            rs_copy(k, level).wait_send()
-            ag_copy(k, level).wait_send()
+        for p in range(2):
+            for level in range(row_bits):
+                rs_copy(k, p, level).wait_send()
+                ag_at(k, p, level, True).wait_send()
     keep_hi.wait()
     keep_lo.wait()
 
@@ -264,13 +283,13 @@
             *pair(), *pair(), *pair(),
             dma((block // TILE,)), dma((chunks,)), dma((2,)),
             dma((chunks, cols_n)), dma((chunks, cols_n)),
-            dma((chunks, row_bits)), dma((chunks, row_bits)),
-            dma((chunks, row_bits)), dma((chunks, row_bits)),
+            dma((chunks, 2, row_bits)), dma((chunks, 2, row_bits)),
+            dma((chunks, 2, row_bits)), dma((chunks, 2, row_bits)),
         ],
         compiler_params=pltpu.CompilerParams(
             collective_id=0, has_side_effects=True, vmem_limit_bytes=60 * 1024 * 1024),
     )(eigvecs, reflectors, tfactors)
-    rows = 256
+    rows = 512
     return pl.pallas_call(
         update_kernel,
         grid=(block // rows,),

time: 115 us -> 104 us (0.904)
  Pallas kernels: 114 us -> 104 us
    pallas_call x1, Pallas kernels: 101 us -> 91.8 us  [local(): pl.pallas_call(functools.partial(reduce_kernel, rows_n, cols_n, cw), out_...]
    pallas_call x1, Pallas kernels: 13.6 us -> 12.2 us  [local(): pl.pallas_call(update_kernel, grid=(block // rows,), out_shape=jax.ShapeD...]
where the time goes in v2:
time: 104 us
  Pallas kernels  104 us (100%)
    pallas_call x1, Pallas kernels, local(): pl.pallas_call(functools.partial(reduce_kernel, rows_n, cols_n, cw), out_...  91.8 us
    pallas_call x1, Pallas kernels, local(): pl.pallas_call(update_kernel, grid=(block // rows,), out_shape=jax.ShapeD...  12.2 us

profile of v2, /device:TPU:0, one launch (start us, length us, event | category | flops | bytes accessed | tf_op | source)
XLA Modules:
  0.0 104.0 jit_solution(1396963371913933373)
XLA Ops:
  0.0 91.8 %shard_map.37 = (bf16[2048,512]{1,0:T(8,128)(2,1)}, bf16[2048,512]{1,0:T(8,128)(2,1)}, bf16[512,1024]{1,0:T(8,128)(2,1)}, bf16[512,1024]{1,0:T(8,128)(2,1)}) custom-call(f32[2048,1024]{1,0:T(8,128)} %eig.3, f32[2,512,256]{2,1,0:T(8,128)} %refl.1, f32[2,256,256]{2,1,0:T(8,128)} %tfac.1), custom_call_target="tpu_custom_call" | custom-call | tf_op jit(solution)/shard_map/pallas_call | solution.py:270
  91.8 12.2 %shard_map.38 = f32[2048,1024]{1,0:T(8,128)} custom-call(f32[2048,1024]{1,0:T(8,128)} %eig.3, bf16[2048,512]{1,0:T(8,128)(2,1)} %get-tuple-element.9.vhi, bf16[2048,512]{1,0:T(8,128)(2,1)} %get-tuple-element.10.vlo, bf16[512,1024]{1,0:T(8,128)(2,1)} %get-tuple-element.11.chi, bf16[512,1024]{1,0:T(8,128)(2,1)} %get-tuple-element.12.clo), custom_call_target="tpu_custom_call" | custom-call | tf_op jit(solution)/shard_map/pallas_call | solution.py:293
